TPU v7x, 128 devices: a whole 4x4x4 slice. The times are simulated.
128 devices in a mesh: sx: 16 (over x, y_lo, core), sy: 8 (over z, y_hi).
Axes of the slice: x: 4, y: 4 (y_hi: 2, y_lo: 2; y = y_hi * 2 + y_lo), z: 4, core: 2. Of those that a mesh axis runs over, the one named last changes fastest.
Arguments:
- queries: bfloat16 [8192, 128, 128], P(('sx', 'sy')), may hold values from -8 to 8
- keys: bfloat16 [8192, 8, 128], P(('sx', 'sy')), may hold values from -8 to 8
- values: bfloat16 [8192, 8, 128], P(('sx', 'sy')), may hold values from -6 to 6
Outputs:
- attention: bfloat16 [8192, 128, 128], P(('sx', 'sy'))
All inputs are finite; a program needn't handle non-finite values.
Results may differ from a plain program's by a relative error of at most 0.005.
Values may be sent and summed in bfloat16 or wider, within the bound.
A program may use at most 64 MiB of HBM per device.

v0:
```python
import math
import jax
import jax.numpy as jnp
from jax import lax
from jax.sharding import PartitionSpec as P


def frequencies(head_width):
    half_index = jnp.arange(head_width // 2, dtype=jnp.float32)
    base_rate = jnp.power(jnp.float32(500000.0), -2.0 * half_index / head_width)
    wavelen = 2.0 * math.pi / base_rate
    smooth = (8192.0 / wavelen - 1.0) / 3.0
    blended = (1.0 - smooth) * base_rate / 8.0 + smooth * base_rate
    return jnp.where(
        wavelen < 2048.0, base_rate, jnp.where(wavelen > 8192.0, base_rate / 8.0, blended)
    )


def rotate(heads_in, positions):
    head_width = heads_in.shape[-1]
    half_width = head_width // 2
    angles = positions.astype(jnp.float32)[:, None] * frequencies(head_width)[None, :]
    cosine = jnp.cos(angles)[:, None, :]
    sine_wave = jnp.sin(angles)[:, None, :]
    widened = heads_in.astype(jnp.float32)
    front = widened[..., :half_width]
    second = widened[..., half_width:]
    turned = jnp.concatenate(
        [front * cosine - second * sine_wave, second * cosine + front * sine_wave], axis=-1
    )
    return turned.astype(jnp.bfloat16)


def attend(query_matrix, block_rows):
    total_rows, head_width = query_matrix.shape
    score_scale = 1.0 / math.sqrt(head_width)
    query_blocks = total_rows // block_rows
    offsets = jnp.arange(block_rows, dtype=jnp.int32)

    def absorb(running, gathered, start_row):
        key_piece = gathered[0][:, 0]
        value_piece = gathered[1][:, 0]
        pieces = key_piece.shape[0] // block_rows
        key_blocks = key_piece.reshape(pieces, block_rows, head_width)
        value_blocks = value_piece.reshape(pieces, block_rows, head_width)
        first_block = start_row // block_rows

        def per_query(query_index, state_now):
            row_max, row_mass, summed = state_now
            row_start = query_index * block_rows
            query_block = lax.dynamic_slice_in_dim(query_matrix, row_start, block_rows, 0)
            query_places = row_start + offsets

            def per_key(key_step, inner_state):
                block_max, block_mass, block_sum = inner_state
                key_block = lax.dynamic_index_in_dim(key_blocks, key_step, 0, keepdims=False)
                value_block = lax.dynamic_index_in_dim(value_blocks, key_step, 0, keepdims=False)
                key_places = start_row + key_step * block_rows + offsets
                scores = (
                    jnp.dot(query_block, key_block.T, preferred_element_type=jnp.float32)
                    * score_scale
                )
                scores = jnp.where(key_places[None, :] <= query_places[:, None], scores, -jnp.inf)
                new_max = jnp.maximum(block_max, jnp.max(scores, axis=1))
                shrink = jnp.exp(block_max - new_max)
                weights = jnp.exp(scores - new_max[:, None])
                block_mass = block_mass * shrink + jnp.sum(weights, axis=1)
                block_sum = block_sum * shrink[:, None] + jnp.dot(
                    weights.astype(jnp.bfloat16), value_block, preferred_element_type=jnp.float32
                )
                return (new_max, block_mass, block_sum)

            key_count = jnp.clip(query_index - first_block + 1, 0, pieces)
            inner_state = (
                lax.dynamic_slice_in_dim(row_max, row_start, block_rows, 0),
                lax.dynamic_slice_in_dim(row_mass, row_start, block_rows, 0),
                lax.dynamic_slice_in_dim(summed, row_start, block_rows, 0),
            )
            block_max, block_mass, block_sum = lax.fori_loop(0, key_count, per_key, inner_state)
            return (
                lax.dynamic_update_slice_in_dim(row_max, block_max, row_start, 0),
                lax.dynamic_update_slice_in_dim(row_mass, block_mass, row_start, 0),
                lax.dynamic_update_slice_in_dim(summed, block_sum, row_start, 0),
            )

        return lax.fori_loop(0, query_blocks, per_query, running)

    return absorb


def shards(queries, keys, values):
    local_rows, heads_all, head_width = queries.shape
    key_heads = keys.shape[1]
    group_size = heads_all // key_heads
    start_row = lax.axis_index(("sx", "sy")) * local_rows
    positions = start_row + jnp.arange(local_rows, dtype=jnp.int32)
    query_rot = rotate(queries, positions)
    key_rot = rotate(keys, positions)
    ordered = (
        query_rot.reshape(local_rows, key_heads, group_size, head_width)
        .transpose(0, 2, 1, 3)
        .reshape(local_rows, heads_all, head_width)
    )
    query_head = lax.all_to_all(ordered, ("sx", "sy"), split_axis=1, concat_axis=0, tiled=True)
    query_matrix = query_head[:, 0]
    block_rows = local_rows * lax.axis_size("sy")
    total_rows = query_matrix.shape[0]
    absorb = attend(query_matrix, block_rows)
    running = (
        jnp.full((total_rows,), -jnp.inf, jnp.float32),
        jnp.zeros((total_rows,), jnp.float32),
        jnp.zeros((total_rows, head_width), jnp.float32),
    )

    def spread(source):
        widened = jnp.broadcast_to(source[:, None], (local_rows, group_size, key_heads, head_width))
        return widened.reshape(local_rows, heads_all, head_width)

    all_keys, all_values = (
        lax.all_to_all(spread(key_rot), ("sx", "sy"), split_axis=1, concat_axis=0, tiled=True),
        lax.all_to_all(spread(values), ("sx", "sy"), split_axis=1, concat_axis=0, tiled=True),
    )
    running = absorb(running, (all_keys, all_values), jnp.zeros((), jnp.int32))
    row_max, row_mass, summed = running
    result = (summed / row_mass[:, None]).astype(jnp.bfloat16)[:, None, :]
    returned = lax.all_to_all(result, ("sx", "sy"), split_axis=0, concat_axis=1, tiled=True)
    attention = (
        returned.reshape(local_rows, group_size, key_heads, head_width)
        .transpose(0, 2, 1, 3)
        .reshape(local_rows, heads_all, head_width)
    )
    return attention


def solution(mesh):
    placed = (P(("sx", "sy"), None, None), P(("sx", "sy"), None, None), P(("sx", "sy"), None, None))
    return jax.shard_map(
        shards, mesh=mesh, in_specs=placed, out_specs=P(("sx", "sy"), None, None), check_vma=False
    )
```

profile of v0, /device:TPU:1, one launch (start us, length us, event | category | flops | bytes accessed | tf_op | source)
XLA Modules:
  0.0 496.9 jit_solution(14280930461415902531)
XLA Ops:
  0.0 4.1 convert_element_type.27
  4.3 5.0 %subtract_convert_fusion = (bf16[64,128,64]{2,1,0:T(8,128)(2,1)S(1)}, bf16[64,128,64]{2,1,0:T(8,128)(2,1)S(1)}) fusion(f32[64,128,128]{2,1,0:T(8,128)} %convert_element_type.27, f32[64,64]{1,0:T(8,128)S(1)} %get-tuple-element.329, f32[64,64]{1,0:T(8,128)S(1)} %get-tuple-element.328), kind=kLoop, calls=%fused_computation.24 | loop fusion | flops 4194304 | bytes 6324224 | tf_op jit(solution)/shard_map/convert.5
  10.5 2.7 copy.20
  13.1 11.5 %all-to-all-start = ((bf16[64,128,128]{2,0,1:T(8,128)(2,1)}), bf16[64,128,128]{2,0,1:T(8,128)(2,1)S(1)}, u32[]{:S(2)}, u32[]{:S(2)}) async-start(bf16[64,128,128]{2,0,1:T(8,128)(2,1)} %bitcast.6), calls=%async_computation | async-start | bytes 4194304 | tf_op jit(solution)/shard_map/all_to_all | solution.py:104
  25.0 30.1 %all-to-all-done = bf16[64,128,128]{2,0,1:T(8,128)(2,1)S(1)} async-done(((bf16[64,128,128]{2,0,1:T(8,128)(2,1)}), bf16[64,128,128]{2,0,1:T(8,128)(2,1)S(1)}, u32[]{:S(2)}, u32[]{:S(2)}) %all-to-all-start) | async-done | bytes 2097184 | tf_op jit(solution)/shard_map/all_to_all | solution.py:104
  57.1 4.8 all-to-all-start.1
  62.0 29.8 %all-to-all-done.1 = bf16[64,128,128]{2,0,1:T(8,128)(2,1)} async-done(((bf16[64,128,128]{2,0,1:T(8,128)(2,1)}), bf16[64,128,128]{2,0,1:T(8,128)(2,1)}, u32[]{:S(2)}, u32[]{:S(2)}) %all-to-all-start.1) | async-done | bytes 2097184 | tf_op jit(solution)/shard_map/all_to_all | solution.py:120
  93.7 3.9 all-to-all-start.2
  97.6 30.5 %all-to-all-done.2 = bf16[64,128,128]{2,0,1:T(8,128)(2,1)S(1)} async-done(((bf16[64,128,128]{2,0,1:T(8,128)(2,1)}), bf16[64,128,128]{2,0,1:T(8,128)(2,1)S(1)}, u32[]{:S(2)}, u32[]{:S(2)}) %all-to-all-start.2) | async-done | bytes 2097184 | tf_op jit(solution)/shard_map/all_to_all | solution.py:121
  130.3 310.3 %while.67 = (s32[]{:T(128)}, f32[8192]{0:T(1024)S(1)}, f32[8192]{0:T(1024)S(1)}, f32[8192,128]{1,0:T(8,128)}, bf16[8192,128]{1,0:T(8,128)(2,1)}, /*index=5*/bf16...) while((s32[]{:T(128)}, f32[8192]{0:T(1024)S(1)}, ...), condition=%wide.region_5.6_spmd.clone.clone, body=%wide.region_0.5_spmd.clone.clone.sunk | while | flops 136448000 | bytes 5435970 | solution.py:86
  137.6 3.8 while.68
  144.7 5.7 %while.68 = (s32[]{:T(128)}, f32[512]{0:T(512)S(1)}, f32[512]{0:T(512)S(1)}, f32[512,128]{1,0:T(8,128)S(1)}, s32[]{:T(128)}, /*index=5*/s32[512]{0:T(512)S(1)}, ...) while((s32[]{:T(128)}, f32[512]{0:T(512)S(1)}, ...), condition=%wide.region_4.4_spmd, body=%wide.region_1.3_spmd.sunk | while | flops 136447488 | bytes 4104391 | solution.py:79
  153.7 7.6 %while.68 = (s32[]{:T(128)}, f32[512]{0:T(512)S(1)}, f32[512]{0:T(512)S(1)}, f32[512,128]{1,0:T(8,128)S(1)}, s32[]{:T(128)}, /*index=5*/s32[512]{0:T(512)S(1)}, ...) while((s32[]{:T(128)}, f32[512]{0:T(512)S(1)}, ...), condition=%wide.region_4.4_spmd, body=%wide.region_1.3_spmd.sunk | while | flops 136447488 | bytes 4104391 | solution.py:79
  164.6 9.5 %while.68 = (s32[]{:T(128)}, f32[512]{0:T(512)S(1)}, f32[512]{0:T(512)S(1)}, f32[512,128]{1,0:T(8,128)S(1)}, s32[]{:T(128)}, /*index=5*/s32[512]{0:T(512)S(1)}, ...) while((s32[]{:T(128)}, f32[512]{0:T(512)S(1)}, ...), condition=%wide.region_4.4_spmd, body=%wide.region_1.3_spmd.sunk | while | flops 136447488 | bytes 4104391 | solution.py:79
  177.4 11.4 %while.68 = (s32[]{:T(128)}, f32[512]{0:T(512)S(1)}, f32[512]{0:T(512)S(1)}, f32[512,128]{1,0:T(8,128)S(1)}, s32[]{:T(128)}, /*index=5*/s32[512]{0:T(512)S(1)}, ...) while((s32[]{:T(128)}, f32[512]{0:T(512)S(1)}, ...), condition=%wide.region_4.4_spmd, body=%wide.region_1.3_spmd.sunk | while | flops 136447488 | bytes 4104391 | solution.py:79
  192.1 13.2 %while.68 = (s32[]{:T(128)}, f32[512]{0:T(512)S(1)}, f32[512]{0:T(512)S(1)}, f32[512,128]{1,0:T(8,128)S(1)}, s32[]{:T(128)}, /*index=5*/s32[512]{0:T(512)S(1)}, ...) while((s32[]{:T(128)}, f32[512]{0:T(512)S(1)}, ...), condition=%wide.region_4.4_spmd, body=%wide.region_1.3_spmd.sunk | while | flops 136447488 | bytes 4104391 | solution.py:79
  208.7 15.1 %while.68 = (s32[]{:T(128)}, f32[512]{0:T(512)S(1)}, f32[512]{0:T(512)S(1)}, f32[512,128]{1,0:T(8,128)S(1)}, s32[]{:T(128)}, /*index=5*/s32[512]{0:T(512)S(1)}, ...) while((s32[]{:T(128)}, f32[512]{0:T(512)S(1)}, ...), condition=%wide.region_4.4_spmd, body=%wide.region_1.3_spmd.sunk | while | flops 136447488 | bytes 4104391 | solution.py:79
  227.1 17.0 %while.68 = (s32[]{:T(128)}, f32[512]{0:T(512)S(1)}, f32[512]{0:T(512)S(1)}, f32[512,128]{1,0:T(8,128)S(1)}, s32[]{:T(128)}, /*index=5*/s32[512]{0:T(512)S(1)}, ...) while((s32[]{:T(128)}, f32[512]{0:T(512)S(1)}, ...), condition=%wide.region_4.4_spmd, body=%wide.region_1.3_spmd.sunk | while | flops 136447488 | bytes 4104391 | solution.py:79
  247.5 18.9 %while.68 = (s32[]{:T(128)}, f32[512]{0:T(512)S(1)}, f32[512]{0:T(512)S(1)}, f32[512,128]{1,0:T(8,128)S(1)}, s32[]{:T(128)}, /*index=5*/s32[512]{0:T(512)S(1)}, ...) while((s32[]{:T(128)}, f32[512]{0:T(512)S(1)}, ...), condition=%wide.region_4.4_spmd, body=%wide.region_1.3_spmd.sunk | while | flops 136447488 | bytes 4104391 | solution.py:79
  269.7 20.8 %while.68 = (s32[]{:T(128)}, f32[512]{0:T(512)S(1)}, f32[512]{0:T(512)S(1)}, f32[512,128]{1,0:T(8,128)S(1)}, s32[]{:T(128)}, /*index=5*/s32[512]{0:T(512)S(1)}, ...) while((s32[]{:T(128)}, f32[512]{0:T(512)S(1)}, ...), condition=%wide.region_4.4_spmd, body=%wide.region_1.3_spmd.sunk | while | flops 136447488 | bytes 4104391 | solution.py:79
  293.8 22.7 %while.68 = (s32[]{:T(128)}, f32[512]{0:T(512)S(1)}, f32[512]{0:T(512)S(1)}, f32[512,128]{1,0:T(8,128)S(1)}, s32[]{:T(128)}, /*index=5*/s32[512]{0:T(512)S(1)}, ...) while((s32[]{:T(128)}, f32[512]{0:T(512)S(1)}, ...), condition=%wide.region_4.4_spmd, body=%wide.region_1.3_spmd.sunk | while | flops 136447488 | bytes 4104391 | solution.py:79
  319.9 24.6 %while.68 = (s32[]{:T(128)}, f32[512]{0:T(512)S(1)}, f32[512]{0:T(512)S(1)}, f32[512,128]{1,0:T(8,128)S(1)}, s32[]{:T(128)}, /*index=5*/s32[512]{0:T(512)S(1)}, ...) while((s32[]{:T(128)}, f32[512]{0:T(512)S(1)}, ...), condition=%wide.region_4.4_spmd, body=%wide.region_1.3_spmd.sunk | while | flops 136447488 | bytes 4104391 | solution.py:79
  347.8 26.5 %while.68 = (s32[]{:T(128)}, f32[512]{0:T(512)S(1)}, f32[512]{0:T(512)S(1)}, f32[512,128]{1,0:T(8,128)S(1)}, s32[]{:T(128)}, /*index=5*/s32[512]{0:T(512)S(1)}, ...) while((s32[]{:T(128)}, f32[512]{0:T(512)S(1)}, ...), condition=%wide.region_4.4_spmd, body=%wide.region_1.3_spmd.sunk | while | flops 136447488 | bytes 4104391 | solution.py:79
  377.6 28.4 %while.68 = (s32[]{:T(128)}, f32[512]{0:T(512)S(1)}, f32[512]{0:T(512)S(1)}, f32[512,128]{1,0:T(8,128)S(1)}, s32[]{:T(128)}, /*index=5*/s32[512]{0:T(512)S(1)}, ...) while((s32[]{:T(128)}, f32[512]{0:T(512)S(1)}, ...), condition=%wide.region_4.4_spmd, body=%wide.region_1.3_spmd.sunk | while | flops 136447488 | bytes 4104391 | solution.py:79
  409.2 30.2 %while.68 = (s32[]{:T(128)}, f32[512]{0:T(512)S(1)}, f32[512]{0:T(512)S(1)}, f32[512,128]{1,0:T(8,128)S(1)}, s32[]{:T(128)}, /*index=5*/s32[512]{0:T(512)S(1)}, ...) while((s32[]{:T(128)}, f32[512]{0:T(512)S(1)}, ...), condition=%wide.region_4.4_spmd, body=%wide.region_1.3_spmd.sunk | while | flops 136447488 | bytes 4104391 | solution.py:79
  440.6 2.9 fusion.14
  444.0 2.8 reduce
  446.8 3.9 reshape.125
  450.7 34.4 %all_to_all.60 = bf16[128,2,4096]{2,1,0:T(2,128)(2,1)S(1)} all-to-all(bf16[128,2,4096]{2,1,0:T(2,128)(2,1)} %reshape.125), channel_id=1, replica_groups=mesh['sx'=16,'sy'=8] {'sx','sy'}, dimensions={0} | all-to-all | bytes 4194304 | tf_op jit(solution)/shard_map/all_to_all | solution.py:126
  485.1 6.7 %reshape.126 = bf16[8192,1,128]{2,1,0:T(2,128)(2,1)} reshape(bf16[128,2,4096]{2,1,0:T(2,128)(2,1)S(1)} %all_to_all.60) | data formatting | bytes 4194304
  491.8 2.5 copy.27
  494.3 2.7 copy.25
  (1118 shorter events, 313.8 us)
Async XLA Ops:
  13.1 11.5 %copy-start.1 = (bf16[64,8,128]{2,1,0:T(8,128)(2,1)S(1)}, bf16[64,8,128]{2,1,0:T(8,128)(2,1)}, u32[]{:S(2)}) copy-start(bf16[64,8,128]{2,1,0:T(8,128)(2,1)} %param.8) | copy-start | bytes 393220
  13.1 42.0 %all-to-all-start = ((bf16[64,128,128]{2,0,1:T(8,128)(2,1)}), bf16[64,128,128]{2,0,1:T(8,128)(2,1)S(1)}, u32[]{:S(2)}, u32[]{:S(2)}) async-start(bf16[64,128,128]{2,0,1:T(8,128)(2,1)} %bitcast.6), calls=%async_computation | async-start | bytes 4194304 | tf_op jit(solution)/shard_map/all_to_all | solution.py:104
  55.1 2.0 copy-start
  57.1 4.9 copy-start.2
  57.1 34.7 %all-to-all-start.1 = ((bf16[64,128,128]{2,0,1:T(8,128)(2,1)}), bf16[64,128,128]{2,0,1:T(8,128)(2,1)}, u32[]{:S(2)}, u32[]{:S(2)}) async-start(bf16[64,128,128]{2,0,1:T(8,128)(2,1)} %bitcast.10), calls=%async_computation.1 | async-start | bytes 4194304 | tf_op jit(solution)/shard_map/all_to_all | solution.py:120
  93.7 34.4 %all-to-all-start.2 = ((bf16[64,128,128]{2,0,1:T(8,128)(2,1)}), bf16[64,128,128]{2,0,1:T(8,128)(2,1)S(1)}, u32[]{:S(2)}, u32[]{:S(2)}) async-start(bf16[64,128,128]{2,0,1:T(8,128)(2,1)} %bitcast.53), calls=%async_computation.2 | async-start | bytes 4194304 | tf_op jit(solution)/shard_map/all_to_all | solution.py:121
where the time goes:
time: 501 us; the launch traced here: 497 us
  matrix products  221 us (44%)
  waiting for transfers between devices  90.4 us (18%)
  local copies, waits for them, and re-layouts  77.7 us (16%)
  other arithmetic  46.4 us (9%)
  blocking collectives  34.4 us (7%)
  starting transfers between devices  20.3 us (4%)
  loops' own time  6.72 us (1%)
    dot_general x136, matrix products, per_key(): jnp.dot(query_block, key_block.T, preferred_element_type=jnp.float32)  167 us
    dot_general x136, matrix products, per_key(): jnp.dot(weights.astype(jnp.bfloat16), value_block, preferred_element_type...  53.9 us
    all_to_all x1, blocking collectives, shards(): lax.all_to_all(result, ('sx', 'sy'), split_axis=0, concat_axis=1, tiled=T...  34.4 us
    all_to_all x1, waiting for transfers between devices, shards(): lax.all_to_all(spread(values), ('sx', 'sy'), split_axis=1, concat_axis=0,...  30.5 us
    all_to_all x1, waiting for transfers between devices, shards(): lax.all_to_all(ordered, ('sx', 'sy'), split_axis=1, concat_axis=0, tiled=...  30.1 us
    all_to_all x1, waiting for transfers between devices, shards(): lax.all_to_all(spread(key_rot), ('sx', 'sy'), split_axis=1, concat_axis=0...  29.8 us
    reduce_sum x136, other arithmetic, per_key(): block_mass = block_mass * shrink + jnp.sum(weights, axis=1)  26.7 us
    dynamic_slice x16, local copies, waits for them, and re-layouts, per_query(): lax.dynamic_slice_in_dim(summed, row_start, block_rows, 0)  15.5 us
  transfers between devices with their start and end apart: 3, of which 3 were waited for; matrix products, arithmetic and copies ran while one was open for 0% of the time, Pallas kernels for 0%

commit v1 on v0

--- a/solution.py
+++ b/solution.py
@@ -123,7 +123,12 @@
     running = absorb(running, (all_keys, all_values), jnp.zeros((), jnp.int32))
     row_max, row_mass, summed = running
     result = (summed / row_mass[:, None]).astype(jnp.bfloat16)[:, None, :]
-    returned = lax.all_to_all(result, ("sx", "sy"), split_axis=0, concat_axis=1, tiled=True)
+    returned = jnp.concatenate(
+        lax.all_to_all(
+            jnp.stack(jnp.split(result, lax.axis_size(("sx", "sy")), axis=0)), ("sx", "sy"), 0, 0
+        ),
+        axis=1,
+    )
     attention = (
         returned.reshape(local_rows, group_size, key_heads, head_width)
         .transpose(0, 2, 1, 3)

time: 501 us -> 474 us (0.946)
  local copies, waits for them, and re-layouts: 77.7 us -> 65.5 us
  other arithmetic: 46.4 us -> 39 us
  waiting for transfers between devices: 90.4 us -> 83.2 us
    unnamed x10 -> x132, local copies, waits for them, and re-layouts: 13.1 us -> 1.22 us
    all_to_all x1, waiting for transfers between devices: 30.5 us -> 23 us  [shards(): lax.all_to_all(spread(values), ('sx', 'sy'), split_axis=1, concat_axis=0,...]
    all_to_all x1, starting transfers between devices: 11.5 us -> 4.71 us  [shards(): lax.all_to_all(ordered, ('sx', 'sy'), split_axis=1, concat_axis=0, tiled=...]
    all_to_all x1, starting transfers between devices: 4.84 us -> 11.5 us  [shards(): lax.all_to_all(spread(key_rot), ('sx', 'sy'), split_axis=1, concat_axis=0...]
    broadcast_in_dim x2 -> x0, other arithmetic: 5.66 us -> none  [shards(): result = (summed / row_mass[:, None]).astype(jnp.bfloat16)[:, None, :]]
  transfers between devices with their start and end apart: 3 -> 3, of which waited for: 3 -> 3; matrix products, arithmetic and copies ran while one was open for 0% -> 2% of each run, Pallas kernels for 0% -> 0%
where the time goes in v1:
time: 474 us; the launch traced here: 471 us
  matrix products  220 us (46%)
  waiting for transfers between devices  83.2 us (18%)
  local copies, waits for them, and re-layouts  65.5 us (14%)
  other arithmetic  39 us (8%)
  blocking collectives  34.2 us (7%)
  starting transfers between devices  20.1 us (4%)
  loops' own time  7.39 us (2%)
    dot_general x136, matrix products, per_key(): jnp.dot(query_block, key_block.T, preferred_element_type=jnp.float32)  167 us
    dot_general x136, matrix products, per_key(): jnp.dot(weights.astype(jnp.bfloat16), value_block, preferred_element_type...  53.4 us
    all_to_all x1, blocking collectives, shards(): lax.all_to_all(jnp.stack(jnp.split(result, lax.axis_size(('sx', 'sy')), a...  34.2 us
    all_to_all x1, waiting for transfers between devices, shards(): lax.all_to_all(spread(key_rot), ('sx', 'sy'), split_axis=1, concat_axis=0...  30.4 us
    all_to_all x1, waiting for transfers between devices, shards(): lax.all_to_all(ordered, ('sx', 'sy'), split_axis=1, concat_axis=0, tiled=...  29.8 us
    reduce_sum x136, other arithmetic, per_key(): block_mass = block_mass * shrink + jnp.sum(weights, axis=1)  26.7 us
    all_to_all x1, waiting for transfers between devices, shards(): lax.all_to_all(spread(values), ('sx', 'sy'), split_axis=1, concat_axis=0,...  23 us
    dynamic_slice x16, local copies, waits for them, and re-layouts, per_query(): lax.dynamic_slice_in_dim(summed, row_start, block_rows, 0)  15.6 us
  transfers between devices with their start and end apart: 3, of which 3 were waited for; matrix products, arithmetic and copies ran while one was open for 2% of the time, Pallas kernels for 0%

profile of v1, /device:TPU:1, one launch (start us, length us, event | category | flops | bytes accessed | tf_op | source)
XLA Modules:
  0.0 470.5 jit_solution(15310732943058141447)
XLA Ops:
  1.5 1.8 broadcast_in_dim.16
  3.3 11.5 %all-to-all-start.1 = ((bf16[64,128,128]{2,0,1:T(8,128)(2,1)}), bf16[64,128,128]{2,0,1:T(8,128)(2,1)S(1)}, u32[]{:S(2)}, u32[]{:S(2)}) async-start(bf16[64,128,128]{2,0,1:T(8,128)(2,1)} %bitcast.10), calls=%async_computation.1 | async-start | bytes 4194304 | tf_op jit(solution)/shard_map/all_to_all | solution.py:120
  14.9 30.4 %all-to-all-done.1 = bf16[64,128,128]{2,0,1:T(8,128)(2,1)S(1)} async-done(((bf16[64,128,128]{2,0,1:T(8,128)(2,1)}), bf16[64,128,128]{2,0,1:T(8,128)(2,1)S(1)}, u32[]{:S(2)}, u32[]{:S(2)}) %all-to-all-start.1) | async-done | bytes 2097184 | tf_op jit(solution)/shard_map/all_to_all | solution.py:120
  45.3 2.0 broadcast_in_dim.17
  47.3 3.9 all-to-all-start.2
  51.2 2.1 convert_element_type.27
  53.3 1.5 subtract_convert_fusion
  56.0 2.7 copy.4
  58.7 23.0 %all-to-all-done.2 = bf16[64,128,128]{2,0,1:T(8,128)(2,1)S(1)} async-done(((bf16[64,128,128]{2,0,1:T(8,128)(2,1)}), bf16[64,128,128]{2,0,1:T(8,128)(2,1)S(1)}, u32[]{:S(2)}, u32[]{:S(2)}) %all-to-all-start.2) | async-done | bytes 2097184 | tf_op jit(solution)/shard_map/all_to_all | solution.py:121
  81.7 4.7 %all-to-all-start = ((bf16[64,128,128]{2,0,1:T(8,128)(2,1)}), bf16[64,128,128]{2,0,1:T(8,128)(2,1)}, u32[]{:S(2)}, u32[]{:S(2)}) async-start(bf16[64,128,128]{2,0,1:T(8,128)(2,1)} %bitcast.561), calls=%async_computation | async-start | bytes 4194304 | tf_op jit(solution)/shard_map/all_to_all | solution.py:104
  86.4 29.8 %all-to-all-done = bf16[64,128,128]{2,0,1:T(8,128)(2,1)} async-done(((bf16[64,128,128]{2,0,1:T(8,128)(2,1)}), bf16[64,128,128]{2,0,1:T(8,128)(2,1)}, u32[]{:S(2)}, u32[]{:S(2)}) %all-to-all-start) | async-done | bytes 2097184 | tf_op jit(solution)/shard_map/all_to_all | solution.py:104
  116.2 2.2 broadcast_in_dim.15
  118.4 310.7 %while.67 = (s32[]{:T(128)}, f32[8192]{0:T(1024)S(1)}, f32[8192]{0:T(1024)S(1)}, f32[8192,128]{1,0:T(8,128)}, bf16[8192,128]{1,0:T(8,128)(2,1)}, /*index=5*/bf16...) while((s32[]{:T(128)}, f32[8192]{0:T(1024)S(1)}, ...), condition=%wide.region_5.6_spmd.clone.clone, body=%wide.region_0.5_spmd.clone.clone.sunk | while | flops 136448000 | bytes 5435962 | solution.py:86
  120.5 1.9 while.68
  125.7 3.8 while.68
  132.8 5.7 %while.68 = (s32[]{:T(128)}, f32[512]{0:T(512)S(1)}, f32[512]{0:T(512)S(1)}, f32[512,128]{1,0:T(8,128)S(1)}, s32[]{:T(128)}, /*index=5*/s32[512]{0:T(512)S(1)}, ...) while((s32[]{:T(128)}, f32[512]{0:T(512)S(1)}, ...), condition=%wide.region_4.4_spmd, body=%wide.region_1.3_spmd.sunk | while | flops 136447488 | bytes 4104391 | solution.py:79
  141.8 7.6 %while.68 = (s32[]{:T(128)}, f32[512]{0:T(512)S(1)}, f32[512]{0:T(512)S(1)}, f32[512,128]{1,0:T(8,128)S(1)}, s32[]{:T(128)}, /*index=5*/s32[512]{0:T(512)S(1)}, ...) while((s32[]{:T(128)}, f32[512]{0:T(512)S(1)}, ...), condition=%wide.region_4.4_spmd, body=%wide.region_1.3_spmd.sunk | while | flops 136447488 | bytes 4104391 | solution.py:79
  152.7 9.5 %while.68 = (s32[]{:T(128)}, f32[512]{0:T(512)S(1)}, f32[512]{0:T(512)S(1)}, f32[512,128]{1,0:T(8,128)S(1)}, s32[]{:T(128)}, /*index=5*/s32[512]{0:T(512)S(1)}, ...) while((s32[]{:T(128)}, f32[512]{0:T(512)S(1)}, ...), condition=%wide.region_4.4_spmd, body=%wide.region_1.3_spmd.sunk | while | flops 136447488 | bytes 4104391 | solution.py:79
  165.5 11.4 %while.68 = (s32[]{:T(128)}, f32[512]{0:T(512)S(1)}, f32[512]{0:T(512)S(1)}, f32[512,128]{1,0:T(8,128)S(1)}, s32[]{:T(128)}, /*index=5*/s32[512]{0:T(512)S(1)}, ...) while((s32[]{:T(128)}, f32[512]{0:T(512)S(1)}, ...), condition=%wide.region_4.4_spmd, body=%wide.region_1.3_spmd.sunk | while | flops 136447488 | bytes 4104391 | solution.py:79
  180.2 13.3 %while.68 = (s32[]{:T(128)}, f32[512]{0:T(512)S(1)}, f32[512]{0:T(512)S(1)}, f32[512,128]{1,0:T(8,128)S(1)}, s32[]{:T(128)}, /*index=5*/s32[512]{0:T(512)S(1)}, ...) while((s32[]{:T(128)}, f32[512]{0:T(512)S(1)}, ...), condition=%wide.region_4.4_spmd, body=%wide.region_1.3_spmd.sunk | while | flops 136447488 | bytes 4104391 | solution.py:79
  196.8 15.2 %while.68 = (s32[]{:T(128)}, f32[512]{0:T(512)S(1)}, f32[512]{0:T(512)S(1)}, f32[512,128]{1,0:T(8,128)S(1)}, s32[]{:T(128)}, /*index=5*/s32[512]{0:T(512)S(1)}, ...) while((s32[]{:T(128)}, f32[512]{0:T(512)S(1)}, ...), condition=%wide.region_4.4_spmd, body=%wide.region_1.3_spmd.sunk | while | flops 136447488 | bytes 4104391 | solution.py:79
  215.3 17.1 %while.68 = (s32[]{:T(128)}, f32[512]{0:T(512)S(1)}, f32[512]{0:T(512)S(1)}, f32[512,128]{1,0:T(8,128)S(1)}, s32[]{:T(128)}, /*index=5*/s32[512]{0:T(512)S(1)}, ...) while((s32[]{:T(128)}, f32[512]{0:T(512)S(1)}, ...), condition=%wide.region_4.4_spmd, body=%wide.region_1.3_spmd.sunk | while | flops 136447488 | bytes 4104391 | solution.py:79
  235.6 19.0 %while.68 = (s32[]{:T(128)}, f32[512]{0:T(512)S(1)}, f32[512]{0:T(512)S(1)}, f32[512,128]{1,0:T(8,128)S(1)}, s32[]{:T(128)}, /*index=5*/s32[512]{0:T(512)S(1)}, ...) while((s32[]{:T(128)}, f32[512]{0:T(512)S(1)}, ...), condition=%wide.region_4.4_spmd, body=%wide.region_1.3_spmd.sunk | while | flops 136447488 | bytes 4104391 | solution.py:79
  257.9 20.9 %while.68 = (s32[]{:T(128)}, f32[512]{0:T(512)S(1)}, f32[512]{0:T(512)S(1)}, f32[512,128]{1,0:T(8,128)S(1)}, s32[]{:T(128)}, /*index=5*/s32[512]{0:T(512)S(1)}, ...) while((s32[]{:T(128)}, f32[512]{0:T(512)S(1)}, ...), condition=%wide.region_4.4_spmd, body=%wide.region_1.3_spmd.sunk | while | flops 136447488 | bytes 4104391 | solution.py:79
  282.1 22.8 %while.68 = (s32[]{:T(128)}, f32[512]{0:T(512)S(1)}, f32[512]{0:T(512)S(1)}, f32[512,128]{1,0:T(8,128)S(1)}, s32[]{:T(128)}, /*index=5*/s32[512]{0:T(512)S(1)}, ...) while((s32[]{:T(128)}, f32[512]{0:T(512)S(1)}, ...), condition=%wide.region_4.4_spmd, body=%wide.region_1.3_spmd.sunk | while | flops 136447488 | bytes 4104391 | solution.py:79
  308.1 24.6 %while.68 = (s32[]{:T(128)}, f32[512]{0:T(512)S(1)}, f32[512]{0:T(512)S(1)}, f32[512,128]{1,0:T(8,128)S(1)}, s32[]{:T(128)}, /*index=5*/s32[512]{0:T(512)S(1)}, ...) while((s32[]{:T(128)}, f32[512]{0:T(512)S(1)}, ...), condition=%wide.region_4.4_spmd, body=%wide.region_1.3_spmd.sunk | while | flops 136447488 | bytes 4104391 | solution.py:79
  336.1 26.5 %while.68 = (s32[]{:T(128)}, f32[512]{0:T(512)S(1)}, f32[512]{0:T(512)S(1)}, f32[512,128]{1,0:T(8,128)S(1)}, s32[]{:T(128)}, /*index=5*/s32[512]{0:T(512)S(1)}, ...) while((s32[]{:T(128)}, f32[512]{0:T(512)S(1)}, ...), condition=%wide.region_4.4_spmd, body=%wide.region_1.3_spmd.sunk | while | flops 136447488 | bytes 4104391 | solution.py:79
  365.9 28.4 %while.68 = (s32[]{:T(128)}, f32[512]{0:T(512)S(1)}, f32[512]{0:T(512)S(1)}, f32[512,128]{1,0:T(8,128)S(1)}, s32[]{:T(128)}, /*index=5*/s32[512]{0:T(512)S(1)}, ...) while((s32[]{:T(128)}, f32[512]{0:T(512)S(1)}, ...), condition=%wide.region_4.4_spmd, body=%wide.region_1.3_spmd.sunk | while | flops 136447488 | bytes 4104391 | solution.py:79
  397.6 30.3 %while.68 = (s32[]{:T(128)}, f32[512]{0:T(512)S(1)}, f32[512]{0:T(512)S(1)}, f32[512,128]{1,0:T(8,128)S(1)}, s32[]{:T(128)}, /*index=5*/s32[512]{0:T(512)S(1)}, ...) while((s32[]{:T(128)}, f32[512]{0:T(512)S(1)}, ...), condition=%wide.region_4.4_spmd, body=%wide.region_1.3_spmd.sunk | while | flops 136447488 | bytes 4104391 | solution.py:79
  429.1 2.9 divide_convert_fusion
  433.7 34.2 %all_to_all.50 = bf16[128,64,1,128]{3,1,2,0:T(8,128)(2,1)S(1)} all-to-all(bf16[128,64,1,128]{3,1,2,0:T(8,128)(2,1)S(1)} %constant_dynamic-update-slice_fusion.1), channel_id=1, replica_groups=mesh['sx'=16,'sy'=8] {'sx','sy'}, dimensions={0} | all-to-all | bytes 4194304 | tf_op jit(solution)/shard_map/all_to_all | solution.py:127
  467.8 2.7 copy.7
  (1239 shorter events, 307.1 us)
Async XLA Ops:
  3.3 11.5 %copy-start.1 = (bf16[64,8,128]{2,1,0:T(8,128)(2,1)S(1)}, bf16[64,8,128]{2,1,0:T(8,128)(2,1)}, u32[]{:S(2)}) copy-start(bf16[64,8,128]{2,1,0:T(8,128)(2,1)} %param.9) | copy-start | bytes 393220
  3.3 42.0 %all-to-all-start.1 = ((bf16[64,128,128]{2,0,1:T(8,128)(2,1)}), bf16[64,128,128]{2,0,1:T(8,128)(2,1)S(1)}, u32[]{:S(2)}, u32[]{:S(2)}) async-start(bf16[64,128,128]{2,0,1:T(8,128)(2,1)} %bitcast.10), calls=%async_computation.1 | async-start | bytes 4194304 | tf_op jit(solution)/shard_map/all_to_all | solution.py:120
  45.3 2.0 copy-start
  47.3 34.4 %all-to-all-start.2 = ((bf16[64,128,128]{2,0,1:T(8,128)(2,1)}), bf16[64,128,128]{2,0,1:T(8,128)(2,1)S(1)}, u32[]{:S(2)}, u32[]{:S(2)}) async-start(bf16[64,128,128]{2,0,1:T(8,128)(2,1)} %bitcast.560), calls=%async_computation.2 | async-start | bytes 4194304 | tf_op jit(solution)/shard_map/all_to_all | solution.py:121
  81.7 34.5 %all-to-all-start = ((bf16[64,128,128]{2,0,1:T(8,128)(2,1)}), bf16[64,128,128]{2,0,1:T(8,128)(2,1)}, u32[]{:S(2)}, u32[]{:S(2)}) async-start(bf16[64,128,128]{2,0,1:T(8,128)(2,1)} %bitcast.561), calls=%async_computation | async-start | bytes 4194304 | tf_op jit(solution)/shard_map/all_to_all | solution.py:104
